TPU v7x, 32 devices: a whole 2x2x4 slice. The times are simulated.
32 devices in a mesh: dp: 2 (over y), row: 4 (over x, core), col: 4 (over z).
Axes of the slice: x: 2, y: 2, z: 4, core: 2. Of those that a mesh axis runs over, the one named last changes fastest.
Arguments:
- tokens: bfloat16 [2048, 8192], P(('dp', 'col'), 'row'), may hold values from -6 to 6
- frozen_weight: bfloat16 [8192, 8192], P('row', 'col'), may hold values from -0.0625 to 0.0625
- input_adapter_factor: bfloat16 [16, 8192], P(None, 'row'), may hold values from -0.0625 to 0.0625
- output_adapter_factor: bfloat16 [16, 8192], P(None, 'col'), may hold values from -1.5 to 1.5
- magnitude: float32 [8192], P('col'), may hold values from 0.5 to 2
- cotangent: bfloat16 [2048, 8192], P(('dp', 'row'), 'col'), may hold values from -6 to 6
- sequence_lengths: int32 [2, 8], P('dp'), may hold values from 1 to 512, 1024 in all within a row
Outputs:
- projected: bfloat16 [2048, 8192], P(('dp', 'row'), 'col')
- grad_mag: float32 [8192], P('col')
- input_factor_gradient: float32 [16, 8192], P(None, 'row')
- grad_b: float32 [16, 8192], P(None, 'col')
Inputs may be any that keep to these rules, and one draw needn't show every extreme that they name: `sequence_lengths`: each group's 8 lengths sum to 1024, and one of them is exactly 512.
All inputs are finite; a program needn't handle non-finite values.
Results may differ from a plain program's by a relative error of at most 0.0052.
Values may be sent and summed in bfloat16 or wider, within the bound.
No kernel may reach another device: no remote copies, remote signals or barrier semaphores. Data moves between devices by JAX's collectives and lax.ppermute only.
A program may use at most 64 MiB of HBM per device.

v0:
```python
import jax
import jax.numpy as jnp
from jax import lax
from jax.sharding import PartitionSpec as P

norm_eps = 1e-06
highest_precision = lax.Precision.HIGHEST


def contract_product(left, right, left_dim, right_dim):
    return lax.dot_general(
        left, right, (((left_dim,), (right_dim,)), ((), ())), preferred_element_type=jnp.float32
    )


def per_device(
    tokens,
    frozen_weight,
    input_adapter_factor,
    output_adapter_factor,
    magnitude,
    cotangent,
    sequence_lengths,
):
    row_count = lax.axis_size("row")
    col_count = lax.axis_size("col")
    row_index = lax.axis_index("row")
    col_index = lax.axis_index("col")
    group_index = lax.axis_index("dp")
    local_rows = tokens.shape[0]
    group_rows = local_rows * col_count
    block_rows = group_rows // row_count
    adapter_rank_size = input_adapter_factor.shape[0]
    low_rank_update = contract_product(input_adapter_factor, output_adapter_factor, 0, 0)
    merged = frozen_weight.astype(jnp.float32) + low_rank_update
    norm_terms = jnp.sum(merged * merged, axis=0)
    gram_partial_terms = contract_product(input_adapter_factor, input_adapter_factor, 1, 1)
    merged_factor_terms = jnp.dot(
        input_adapter_factor, frozen_weight, preferred_element_type=jnp.float32
    ) + jnp.dot(
        gram_partial_terms, output_adapter_factor.astype(jnp.float32), precision=highest_precision
    )
    portion = lax.all_gather(tokens, "col", axis=0, tiled=True)
    base_piece = jnp.dot(portion, frozen_weight, preferred_element_type=jnp.float32)
    down_portion = contract_product(portion, input_adapter_factor, 1, 1)
    frozen_rows, down_rows = (
        lax.psum_scatter(base_piece, "row", scatter_dimension=0, tiled=True),
        lax.psum_scatter(down_portion, "row", scatter_dimension=0, tiled=True),
    )
    norm_sq, merged_input_factor = lax.psum((norm_terms, merged_factor_terms), "row")
    down_activations = down_rows.astype(jnp.bfloat16)
    col_norm = jnp.sqrt(norm_sq + norm_eps)
    col_scale = magnitude / col_norm
    query_projection = frozen_rows + jnp.dot(
        down_activations, output_adapter_factor, preferred_element_type=jnp.float32
    )
    projected = (query_projection * col_scale[None, :]).astype(jnp.bfloat16)
    lengths = sequence_lengths[0]
    ends = jnp.cumsum(lengths, dtype=jnp.int32)
    starts = ends - lengths
    positions = row_index * block_rows + jnp.arange(block_rows, dtype=jnp.int32)
    inside = (positions[:, None] >= starts[None, :]) & (positions[:, None] < ends[None, :])
    inverse = 1.0 / lengths.astype(jnp.float32)
    weights = jnp.sum(jnp.where(inside, inverse[None, :], jnp.float32(0.0)), axis=1)
    grad_out = cotangent.astype(jnp.float32) * weights[:, None]
    scale_terms = jnp.sum(grad_out * query_projection, axis=0)
    projection_gradient = (grad_out * col_scale[None, :]).astype(jnp.bfloat16)
    bgrad_terms = contract_product(down_activations, projection_gradient, 0, 0)
    scale_grad, bgrad_data = lax.psum((scale_terms, bgrad_terms), ("dp", "row"))
    grad_mag = scale_grad / col_norm
    norm_coefficient = -scale_grad * magnitude / (col_norm * col_norm * col_norm)
    grad_b = bgrad_data + merged_input_factor * norm_coefficient[None, :]
    backward_terms = contract_product(projection_gradient, output_adapter_factor, 1, 1)
    padded = lax.dynamic_update_slice_in_dim(
        jnp.zeros((group_rows, adapter_rank_size), jnp.float32),
        backward_terms,
        row_index * block_rows,
        0,
    )
    backward_rows = lax.psum(padded, ("row", "col")).astype(jnp.bfloat16)
    back_mine = lax.dynamic_slice_in_dim(backward_rows, col_index * local_rows, local_rows, 0)
    row_term = contract_product(back_mine, tokens, 0, 0)
    scaled_output_factor = (
        output_adapter_factor.astype(jnp.float32) * norm_coefficient[None, :]
    ).astype(jnp.bfloat16)
    norm_term = contract_product(scaled_output_factor, frozen_weight, 1, 1) + jnp.dot(
        contract_product(scaled_output_factor, output_adapter_factor, 1, 1),
        input_adapter_factor.astype(jnp.float32),
        precision=highest_precision,
    )
    first_group = (group_index == 0).astype(jnp.float32)
    input_factor_gradient = lax.psum(row_term + first_group * norm_term, ("dp", "col"))
    return (projected, grad_mag, input_factor_gradient, grad_b)


def solution(mesh):
    in_specs = (
        P(("dp", "col"), "row"),
        P("row", "col"),
        P(None, "row"),
        P(None, "col"),
        P("col"),
        P(("dp", "row"), "col"),
        P("dp", None),
    )
    out_specs = (P(("dp", "row"), "col"), P("col"), P(None, "row"), P(None, "col"))
    return jax.shard_map(
        per_device, mesh=mesh, in_specs=in_specs, out_specs=out_specs, check_vma=False
    )
```

profile of v0, /device:TPU:0, one launch (start us, length us, event | category | flops | bytes accessed | tf_op | source)
XLA Modules:
  0.0 366.2 jit_solution(13270679273868545477)
XLA Ops:
  7.2 0.0 copy-start
  7.2 0.0 all-gather.2.cloned.1.call-start
  7.2 0.7 all-gather.2.cloned.1.call-update
  7.9 0.0 reduce-scatter.5.cloned.1.call-start
  8.0 85.1 %all-gather.2.cloned.1.call-done = bf16[1024,2048]{1,0:T(8,128)(2,1)} async-done(((bf16[256,2048]{1,0:T(8,128)(2,1)}), bf16[1024,2048]{1,0:T(8,128)(2,1)}) %all-gather.2.cloned.1.call-update) | async-done | bytes 4194320 | tf_op jit(solution)/shard_map/all_gather | solution.py:43
  93.1 0.0 copy-done
  93.1 4.0 %fusion.14 = f32[1024,16]{0,1:T(8,128)} fusion(bf16[1024,2048]{1,0:T(8,128)(2,1)} %all-gather.2.cloned.1.call-done, bf16[16,2048]{1,0:T(8,128)(2,1)S(1)} %copy-done), kind=kOutput, calls=%fused_computation.33 | convolution fusion | flops 67108864 | bytes 4325376 | tf_op jit(solution)/shard_map/dot_general | solution.py:11
  97.1 0.0 reduce-scatter.5.cloned.1.call-update
  97.1 0.0 reduce-scatter.3.cloned.1.call-start
  97.1 14.4 %fusion.13 = f32[1024,2048]{1,0:T(8,128)} fusion(bf16[1024,2048]{1,0:T(8,128)(2,1)} %all-gather.2.cloned.1.call-done, bf16[2048,2048]{1,0:T(8,128)(2,1)} %param.8), kind=kOutput, calls=%fused_computation.32 | convolution fusion | flops 8589934592 | bytes 20971520 | tf_op jit(solution)/shard_map/dot_general | solution.py:44
  111.6 0.0 reduce-scatter.3.cloned.1.call-update
  111.6 0.0 all-reduce.8.cloned.1.call-start
  111.6 0.1 fusion.16
  111.8 4.6 %fusion.15 = f32[16,2048]{1,0:T(8,128)S(1)} fusion(bf16[16,2048]{1,0:T(8,128)(2,1)S(1)} %copy-done, bf16[2048,2048]{1,0:T(8,128)(2,1)} %param.8), kind=kOutput, calls=%fused_computation.34 | convolution fusion | flops 134217728 | bytes 8585216 | tf_op jit(solution)/shard_map/dot_general | solution.py:38
  116.4 0.0 copy-done.2
  116.4 0.9 convolution_add_fusion.1
  117.3 0.0 all-reduce.8.cloned.1.call-update
  117.3 0.0 all-reduce.6.cloned.1.call-start
  117.3 0.0 copy-start.5
  117.4 0.0 copy-start.4
  117.4 0.0 copy-start.3
  117.4 5.9 %multiply_reduce_fusion = f32[2048]{0:T(1024)S(1)} fusion(bf16[2048,2048]{1,0:T(8,128)(2,1)} %param.8, bf16[16,2048]{1,0:T(8,128)(2,1)S(1)} %copy-done, bf16[16,2048]{1,0:T(8,128)(2,1)S(1)} %copy-done.2), kind=kOutput, calls=%fused_computation | convolution fusion | flops 150992896 | bytes 8527872 | tf_op jit(solution)/shard_map/dot_general | solution.py:11
  123.3 0.0 copy-done.5
  123.3 0.2 reduce-window.4
  123.5 6.5 %psum.42 = f32[2048]{0:T(1024)S(1)} all-reduce(f32[2048]{0:T(1024)S(1)} %multiply_reduce_fusion), channel_id=1, replica_groups=mesh['dp'=2,'row'=4,'col'=4] {'row'}, use_global_device_ids=true, to_apply=%region_3.0 | all-reduce | flops 2048 | bytes 16384 | tf_op jit(solution)/shard_map/psum | solution.py:50
  130.0 0.0 copy-done.4
  130.1 0.1 select_reduce_fusion
  130.2 0.5 convolution_dynamic-update-slice_fusion
  130.7 69.2 %psum.44 = bf16[1024,16]{1,0:T(8,128)(2,1)S(1)} all-reduce(f32[1024,16]{1,0:T(8,128)S(1)} %convolution_dynamic-update-slice_fusion), channel_id=1, replica_groups=mesh['dp'=2,'row'=4,'col'=4] {'row','col'}, use_global_device_ids=true, to_apply=%region_8.9 | all-reduce | flops 16384 | bytes 98304 | tf_op jit(solution)/shard_map/psum | solution.py:80
  199.9 0.0 reduce-scatter.5.cloned.1.call-done
  200.0 1.8 fusion.1
  201.8 0.0 all-reduce.6.cloned.1.call-update
  201.8 0.0 all-reduce.4.cloned.1.call-start
  201.8 0.0 reduce-scatter.3.cloned.1.call-done
  201.9 3.2 multiply_reduce_fusion.1
  205.1 12.1 %psum.43 = f32[2048]{0:T(1024)S(1)} all-reduce(f32[2048]{0:T(1024)S(1)} %get-tuple-element.4), channel_id=1, replica_groups=mesh['dp'=2,'row'=4,'col'=4] {'dp','row'}, use_global_device_ids=true, to_apply=%region_7.8 | all-reduce | flops 2048 | bytes 16384 | tf_op jit(solution)/shard_map/psum | solution.py:69
  217.1 0.6 fusion.6
  217.8 5.7 %fusion.3 = f32[16,2048]{1,0:T(8,128)S(1)} fusion(bf16[2048,2048]{1,0:T(8,128)(2,1)} %param.8, bf16[16,2048]{1,0:T(8,128)(2,1)S(1)} %copy-done.2, f32[2048]{0:T(1024)S(1)} %get-tuple-element.6), kind=kOutput, calls=%fused_computation.16 | convolution fusion | flops 134316032 | bytes 8593408 | tf_op jit(solution)/shard_map/dot_general | solution.py:11
  223.5 0.1 fusion.2
  223.6 0.2 fusion
  223.9 0.0 copy-done.1
  223.9 0.9 convolution_add_fusion.3
  224.8 0.0 all-reduce.4.cloned.1.call-update
  224.8 2.4 all-reduce.8.cloned.1.call-done
  227.2 57.0 %all-reduce.6.cloned.1.call-done = f32[16,2048]{1,0:T(8,128)} async-done(((f32[16,2048]{1,0:T(8,128)}), f32[16,2048]{1,0:T(8,128)}) %all-reduce.6.cloned.1.call-update) | async-done | bytes 131088 | tf_op jit(solution)/shard_map/psum | solution.py:69
  284.2 1.6 multiply_add_fusion
  285.9 71.9 %all-reduce.4.cloned.1.call-done = f32[16,2048]{1,0:T(8,128)} async-done(((f32[16,2048]{1,0:T(8,128)}), f32[16,2048]{1,0:T(8,128)}) %all-reduce.4.cloned.1.call-update) | async-done | bytes 131088 | tf_op jit(solution)/shard_map/psum | solution.py:92
  357.8 1.6 copy.15
  (8 shorter events, 0.1 us)
Async XLA Ops:
  7.2 85.9 %copy-start = (bf16[16,2048]{1,0:T(8,128)(2,1)S(1)}, bf16[16,2048]{1,0:T(8,128)(2,1)}, u32[]{:S(2)}) copy-start(bf16[16,2048]{1,0:T(8,128)(2,1)} %param.9) | copy-start | bytes 196612
  7.2 85.9 %all-gather.2.cloned.1.call-start = ((), (), s32[]{:S(2)}) async-start(), calls=%async_computation.2 | async-start | bytes 5242880 | tf_op jit(solution)/shard_map/all_gather | solution.py:43
  7.9 192.0 %reduce-scatter.5.cloned.1.call-start = ((), (), s32[]{:S(2)}) async-start(), calls=%async_computation.4 | async-start | bytes 81920 | tf_op jit(solution)/shard_map/reduce_scatter | solution.py:48
  97.1 104.8 %reduce-scatter.3.cloned.1.call-start = ((), (), s32[]{:S(2)}) async-start(), calls=%async_computation.3 | async-start | bytes 10485760 | tf_op jit(solution)/shard_map/reduce_scatter | solution.py:47
  111.6 115.7 %all-reduce.8.cloned.1.call-start = ((), (), s32[]{:S(2)}) async-start(), calls=%async_computation.7 | async-start | bytes 262144 | tf_op jit(solution)/shard_map/psum | solution.py:50
  111.8 4.6 %copy-start.2 = (bf16[16,2048]{1,0:T(8,128)(2,1)S(1)}, bf16[16,2048]{1,0:T(8,128)(2,1)}, u32[]{:S(2)}) copy-start(bf16[16,2048]{1,0:T(8,128)(2,1)} %param.10) | copy-start | bytes 196612
  117.3 166.9 %all-reduce.6.cloned.1.call-start = ((), (), s32[]{:S(2)}) async-start(), calls=%async_computation.6 | async-start | bytes 262144 | tf_op jit(solution)/shard_map/psum | solution.py:69
  117.3 5.9 %copy-start.5 = (s32[1,8]{1,0:T(1,128)S(1)}, s32[1,8]{1,0:T(1,128)}, u32[]{:S(2)}) copy-start(s32[1,8]{1,0:T(1,128)} %param.13) | copy-start | bytes 100
  117.4 12.7 %copy-start.4 = (f32[2048]{0:T(1024)S(1)}, f32[2048]{0:T(1024)}, u32[]{:S(2)}) copy-start(f32[2048]{0:T(1024)} %param.11) | copy-start | bytes 24580
  117.4 12.8 %copy-start.3 = (bf16[256,2048]{1,0:T(8,128)(2,1)S(1)}, bf16[256,2048]{1,0:T(8,128)(2,1)}, u32[]{:S(2)}) copy-start(bf16[256,2048]{1,0:T(8,128)(2,1)} %param.12) | copy-start | bytes 3145732
  201.8 156.0 %all-reduce.4.cloned.1.call-start = ((), (), s32[]{:S(2)}) async-start(), calls=%async_computation.5 | async-start | bytes 262144 | tf_op jit(solution)/shard_map/psum | solution.py:92
  217.8 6.1 %copy-start.1 = (bf16[256,2048]{1,0:T(8,128)(2,1)S(1)}, bf16[256,2048]{1,0:T(8,128)(2,1)}, u32[]{:S(2)}) copy-start(bf16[256,2048]{1,0:T(8,128)(2,1)} %param.7) | copy-start | bytes 3145732
Sparse Core Ops, SparseCore 0:
  9.6 83.4 all-gather.1
  97.2 18.0 reduce-scatter.4
  117.9 75.6 reduce-scatter.2
  195.8 31.4 all-reduce.7
  230.7 53.4 all-reduce.5
  288.0 69.7 all-reduce.3
where the time goes:
time: 367 us; the launch traced here: 366 us
  waiting for transfers between devices  217 us (59%)
  blocking collectives  87.8 us (24%)
  matrix products  42.5 us (12%)
  between operations  14.3 us (4%)
    all_gather x1, waiting for transfers between devices, per_device(): portion = lax.all_gather(tokens, 'col', axis=0, tiled=True)  85.1 us
    psum x1, waiting for transfers between devices, per_device(): lax.psum(row_term + first_group * norm_term, ('dp', 'col'))  71.9 us
    psum x1, blocking collectives, per_device(): backward_rows = lax.psum(padded, ('row', 'col')).astype(jnp.bfloat16)  69.2 us
    psum x1, waiting for transfers between devices, per_device(): scale_grad, bgrad_data = lax.psum((scale_terms, bgrad_terms), ('dp', 'row'))  57 us
    dot_general x8, matrix products, contract_product(): lax.dot_general(left, right, (((left_dim,), (right_dim,)), ((), ())), pre...  19.1 us
    dot_general x1, matrix products, per_device(): jnp.dot(portion, frozen_weight, preferred_element_type=jnp.float32)  14.4 us
    psum x1, blocking collectives, per_device(): scale_grad, bgrad_data = lax.psum((scale_terms, bgrad_terms), ('dp', 'row'))  12.1 us
  transfers between devices with their start and end apart: 6, of which 4 were waited for; matrix products, arithmetic and copies ran while one was open for 11% of the time, Pallas kernels for 0%

commit v1 on v0

v1 whole, which is shorter than its diff:
```python
import functools

import jax
import jax.numpy as jnp
from jax import lax
from jax.experimental import pallas as pl
from jax.experimental.pallas import tpu as pltpu
from jax.sharding import PartitionSpec as P

norm_eps = 1e-06
highest_precision = lax.Precision.HIGHEST
chunk_rows = 128
column_tile = 1024
kernel_memory = 28 << 20


def contract_product(left, right, left_dim, right_dim):
    return lax.dot_general(
        left, right, (((left_dim,), (right_dim,)), ((), ())), preferred_element_type=jnp.float32
    )


def exchange(value, axis, bit):
    pairs = [(i, i ^ bit) for i in range(lax.axis_size(axis))]
    return lax.ppermute(value, axis, pairs)


def bits_of(axis):
    bits = []
    while (1 << len(bits)) < lax.axis_size(axis):
        bits.append(1 << len(bits))
    return bits


def all_sum(value, axis):
    for bit in bits_of(axis):
        value = value + exchange(value, axis, bit)
    return value


def all_sum_narrow(value, axis):
    for bit in bits_of(axis):
        mine = value.astype(jnp.bfloat16)
        other = exchange(mine, axis, bit)
        value = mine.astype(jnp.float32) + other.astype(jnp.float32)
    return value


def reversed_bits(value, count):
    result, size = 0, count
    while size > 1:
        result = result * 2 + (value & 1)
        value = value >> 1
        size //= 2
    return result


def prepare_kernel(weight_ref, down_ref, up_ref, norm_ref, merged_ref, gram_ref):
    features = weight_ref.shape[0]
    down = down_ref[...]
    up = up_ref[...]

    @pl.when(pl.program_id(0) == 0)
    def _():
        gram_ref[...] = contract_product(down, down, 1, 1)

    merged_ref[...] = jnp.dot(
        down, weight_ref[...], preferred_element_type=jnp.float32
    ) + jnp.dot(
        gram_ref[...],
        up.astype(jnp.float32),
        precision=highest_precision,
        preferred_element_type=jnp.float32,
    )
    step = min(256, features)
    total = jnp.zeros((1, up.shape[1]), jnp.float32)
    for start in range(0, features, step):
        merged = weight_ref[start : start + step, :].astype(jnp.float32) + contract_product(
            down[:, start : start + step], up, 0, 0
        )
        total = total + jnp.sum(merged * merged, axis=0, keepdims=True)
    norm_ref[...] = total


def prepare(weight, down, up):
    features, columns = weight.shape
    rank = down.shape[0]
    tile = min(column_tile, columns)
    return pl.pallas_call(
        prepare_kernel,
        grid=(columns // tile,),
        in_specs=[
            pl.BlockSpec((features, tile), lambda j: (0, j)),
            pl.BlockSpec((rank, features), lambda j: (0, 0)),
            pl.BlockSpec((rank, tile), lambda j: (0, j)),
        ],
        out_specs=[
            pl.BlockSpec((1, tile), lambda j: (0, j)),
            pl.BlockSpec((rank, tile), lambda j: (0, j)),
        ],
        out_shape=[
            jax.ShapeDtypeStruct((1, columns), jnp.float32),
            jax.ShapeDtypeStruct((rank, columns), jnp.float32),
        ],
        scratch_shapes=[pltpu.VMEM((rank, rank), jnp.float32)],
        cost_estimate=pl.CostEstimate(
            flops=6_000_000_000, bytes_accessed=2 * features * columns, transcendentals=0
        ),
        compiler_params=pltpu.CompilerParams(vmem_limit_bytes=kernel_memory),
        name="prepare",
    )(weight, down, up)


def block_kernel(at, choices, parts, first, *refs):
    entry, piece_index, pieces = at
    refs = list(refs)
    place_ref, length_ref = refs.pop(0), refs.pop(0)
    sources = [[refs.pop(0) for _ in range(parts)] for _ in range(choices)]
    weight_ref, down_ref, up_ref, scale_ref = (refs.pop(0) for _ in range(4))
    cotangents = [refs.pop(0) for _ in range(parts)]
    if not first:
        scale_in, grad_in, row_in = (refs.pop(0) for _ in range(3))
        del refs[:parts]
    partials = [refs.pop(0) for _ in range(parts)]
    scale_out, grad_out, row_out = (refs.pop(0) for _ in range(3))
    rows_ref, share_ref, acts_ref, acts_t_ref, back_ref, sem = refs
    step = pl.program_id(0)
    count = sources[0][0].shape[0]

    @pl.when(step == 0)
    def _():
        for c in range(choices):

            @pl.when(place_ref[entry + 1] == c)
            def _(c=c):
                for p in range(parts):
                    copy = pltpu.make_async_copy(
                        sources[c][p], rows_ref.at[pl.ds(p * count, count)], sem
                    )
                    copy.start()
                    copy.wait()

        base = (place_ref[entry + 2] * pieces + piece_index) * count
        position = base + lax.broadcasted_iota(jnp.int32, share_ref.shape, 0)
        length = jnp.zeros(share_ref.shape, jnp.int32)
        end = jnp.int32(0)
        for q in range(length_ref.shape[0]):
            start, end = end, end + length_ref[q]
            inside = (position >= start) & (position < end)
            length = jnp.where(inside, length_ref[q], length)
        share_ref[...] = 1.0 / length.astype(jnp.float32)
        rows = rows_ref[...]
        acts_ref[...] = contract_product(rows, down_ref[...], 1, 1).astype(jnp.bfloat16)
        acts_t_ref[...] = contract_product(down_ref[...], rows, 1, 1).astype(jnp.bfloat16)
        back_ref[...] = jnp.zeros_like(back_ref)

    up = up_ref[...]
    partial = jnp.dot(
        rows_ref[...], weight_ref[...], preferred_element_type=jnp.float32
    ) + jnp.dot(acts_ref[...], up, preferred_element_type=jnp.float32)
    scale = scale_ref[...]
    scale_sum = jnp.zeros_like(scale_out) if first else scale_in[...]
    grads = []
    for p in range(parts):
        piece = partial[p * count : (p + 1) * count]
        weighted = cotangents[p][0].astype(jnp.float32) * share_ref[p * count : (p + 1) * count]
        scale_sum = scale_sum + jnp.sum(weighted * piece, axis=0, keepdims=True)
        grads.append((weighted * scale).astype(jnp.bfloat16))
        partials[p][0] = piece.astype(jnp.bfloat16)
    scale_out[...] = scale_sum
    grad = grads[0] if parts == 1 else jnp.concatenate(grads, axis=0)
    grad_sum = jnp.dot(acts_t_ref[...], grad, preferred_element_type=jnp.float32)
    grad_out[...] = grad_sum if first else grad_in[...] + grad_sum
    back_ref[...] += contract_product(up, grad, 1, 1)

    @pl.when(step == pl.num_programs(0) - 1)
    def _():
        row_sum = jnp.dot(
            back_ref[...].astype(jnp.bfloat16),
            rows_ref[...],
            preferred_element_type=jnp.float32,
        )
        row_out[...] = row_sum if first else row_in[...] + row_sum


def block_step(at, scalars, sources, weight, down, up, scale, cotangents, sums):
    features, columns = weight.shape
    rank = down.shape[0]
    parts = len(cotangents)
    slots, count, _ = cotangents[0].shape
    tile = min(column_tile, columns)
    first = sums is None
    choices = len(sources)
    rows = parts * count
    moving = pl.BlockSpec((1, count, tile), lambda j, place, _: (place[at[0]], 0, j))
    wide = pl.BlockSpec((rank, tile), lambda j, *_: (0, j))
    line = pl.BlockSpec((1, tile), lambda j, *_: (0, j))
    whole = pl.BlockSpec((rank, features), lambda j, *_: (0, 0))
    in_specs = [pl.BlockSpec(memory_space=pl.ANY)] * (choices * parts)
    in_specs += [pl.BlockSpec((features, tile), lambda j, *_: (0, j)), whole, wide, line]
    in_specs += [moving] * parts
    operands = [piece for source in sources for piece in source]
    operands += [weight, down, up, scale, *cotangents]
    aliases = {}
    if not first:
        base = len(scalars) + len(operands)
        in_specs += [line, wide, whole] + [pl.BlockSpec(memory_space=pl.ANY)] * parts
        operands += [*sums[1:], *sums[0]]
        aliases = {base: parts, base + 1: parts + 1, base + 2: parts + 2}
        aliases.update({base + 3 + p: p for p in range(parts)})
    results = pl.pallas_call(
        functools.partial(block_kernel, at, choices, parts, first),
        grid_spec=pltpu.PrefetchScalarGridSpec(
            num_scalar_prefetch=len(scalars),
            grid=(columns // tile,),
            in_specs=in_specs,
            out_specs=[moving] * parts + [line, wide, whole],
            scratch_shapes=[
                pltpu.VMEM((rows, features), jnp.bfloat16),
                pltpu.VMEM((rows, 1), jnp.float32),
                pltpu.VMEM((rows, rank), jnp.bfloat16),
                pltpu.VMEM((rank, rows), jnp.bfloat16),
                pltpu.VMEM((rank, rows), jnp.float32),
                pltpu.SemaphoreType.DMA,
            ],
        ),
        out_shape=[jax.ShapeDtypeStruct((slots, count, columns), jnp.bfloat16)] * parts
        + [
            jax.ShapeDtypeStruct((1, columns), jnp.float32),
            jax.ShapeDtypeStruct((rank, columns), jnp.float32),
            jax.ShapeDtypeStruct((rank, features), jnp.float32),
        ],
        input_output_aliases=aliases,
        cost_estimate=pl.CostEstimate(
            flops=2 * rows * features * columns,
            bytes_accessed=2 * features * columns,
            transcendentals=0,
        ),
        compiler_params=pltpu.CompilerParams(vmem_limit_bytes=kernel_memory),
    )(*scalars, *operands)
    return (results[:parts], *results[parts:])


def chain_steps(pieces):
    count = lax.axis_size("col")
    even, odd = [pieces], [pieces]
    for step in range(1, count):
        arrived = []
        for parity, source in ((0, odd), (1, even)):
            pairs = []
            for i in range(parity, count - 1, 2):
                if i >= step - 1:
                    pairs.append((i, i + 1))
                if i <= count - 1 - step:
                    pairs.append((i + 1, i))
            moved = None
            if pairs:
                moved = []
                for piece in source[-1]:
                    moved.append(lax.ppermute(piece, "col", pairs))
            arrived.append(moved)
        even.append(arrived[0])
        odd.append(arrived[1])
    return even, odd


def arrival_order(count):
    order = []
    for place in range(count):
        left = [(step, 1 - place % 2, place - step) for step in range(1, place + 1)]
        right = [(step, place % 2, place + step) for step in range(1, count - place)]
        order.append(sorted(left + right))
    return order


def per_device(
    tokens,
    frozen_weight,
    input_adapter_factor,
    output_adapter_factor,
    magnitude,
    cotangent,
    sequence_lengths,
):
    row_count = lax.axis_size("row")
    col_count = lax.axis_size("col")
    row_index = lax.axis_index("row")
    col_index = lax.axis_index("col")
    local_rows, _ = tokens.shape
    columns = frozen_weight.shape[1]
    block_rows = local_rows * col_count // row_count
    per_slot = col_count // row_count
    pieces = max(1, local_rows // chunk_rows)
    count = local_rows // pieces

    token_pieces = [tokens[k * count : (k + 1) * count] for k in range(pieces)]
    chains = chain_steps(token_pieces)

    own_cotangent = cotangent.reshape(per_slot, pieces, count, columns)
    cotangents = []
    for k in range(pieces):
        held = own_cotangent[:, k]
        for bit in reversed(bits_of("row")):
            held = jnp.concatenate([held, exchange(held, "row", bit)], axis=0)
        cotangents.append(held)

    norm_terms, merged_factor_terms = prepare(
        frozen_weight, input_adapter_factor, output_adapter_factor
    )
    norm_sq = all_sum(norm_terms, "row")
    col_norm = jnp.sqrt(norm_sq + norm_eps)
    magnitude = magnitude[None, :]
    col_scale = magnitude / col_norm

    order = arrival_order(col_count)
    choices, table = [[None]], [[[place, 0] for place in range(col_count)]]
    for step in range(1, col_count):
        arrivals = [order[place][step - 1] for place in range(col_count)]
        choices.append(sorted({arrival[:2] for arrival in arrivals}))
        table.append([[a[2], choices[-1].index(a[:2])] for a in arrivals])
    table = jnp.array(table, jnp.int32)
    here = lax.dynamic_index_in_dim(table, col_index, 1, keepdims=False)
    blocks = here[:, 0]
    slot = reversed_bits(lax.div(blocks, jnp.int32(per_slot)) ^ row_index, row_count)
    slot = slot * per_slot + lax.rem(blocks, jnp.int32(per_slot))
    places = jnp.stack([slot, here[:, 1], blocks], axis=1).reshape(-1)

    sums = None
    fixed = (frozen_weight, input_adapter_factor, output_adapter_factor, col_scale)
    for step in range(col_count):
        groups = [[k] for k in range(pieces)] if step == col_count - 1 else [list(range(pieces))]
        for group in groups:
            sources = [token_pieces if c is None else chains[c[1]][c[0]] for c in choices[step]]
            sources = [[source[k] for k in group] for source in sources]
            previous = None
            if sums is not None:
                previous = ([sums[0][k] for k in group], *sums[1:])
            result = block_step(
                (3 * step, group[0], pieces),
                (places, sequence_lengths[0]),
                sources,
                *fixed,
                [cotangents[k] for k in group],
                previous,
            )
            partials = [None] * pieces if sums is None else list(sums[0])
            for k, partial in zip(group, result[0]):
                partials[k] = partial
            sums = (partials, *result[1:])
    partials, scale_terms, bgrad_terms, row_term = sums

    outputs = []
    for k in range(pieces):
        held = partials[k]
        for bit in bits_of("row"):
            half = held.shape[0] // 2
            received = exchange(held[half:], "row", bit)
            held = held[:half].astype(jnp.float32) + received.astype(jnp.float32)
            if held.shape[0] > per_slot:
                held = held.astype(jnp.bfloat16)
        outputs.append((held.astype(jnp.float32) * col_scale).astype(jnp.bfloat16))
    projected = jnp.stack(outputs, axis=1).reshape(block_rows, columns)

    scale_grad = all_sum(all_sum(scale_terms, "row"), "dp")
    grad_mag = scale_grad / col_norm
    norm_coefficient = -scale_grad * magnitude / (col_norm * col_norm * col_norm)
    scaled_output_factor = (
        output_adapter_factor.astype(jnp.float32) * norm_coefficient
    ).astype(jnp.bfloat16)
    norm_term = contract_product(scaled_output_factor, frozen_weight, 1, 1) + jnp.dot(
        contract_product(scaled_output_factor, output_adapter_factor, 1, 1),
        input_adapter_factor.astype(jnp.float32),
        precision=highest_precision,
    )
    row_term = all_sum(row_term, "dp")
    input_factor_gradient = all_sum_narrow(row_term + norm_term, "col")

    share = 1.0 / lax.axis_size("dp")
    grad_b = bgrad_terms + merged_factor_terms * (norm_coefficient * share)
    grad_b = all_sum(all_sum(grad_b, "row"), "dp")
    return (projected, grad_mag[0], input_factor_gradient, grad_b)


def solution(mesh):
    in_specs = (
        P(("dp", "col"), "row"),
        P("row", "col"),
        P(None, "row"),
        P(None, "col"),
        P("col"),
        P(("dp", "row"), "col"),
        P("dp", None),
    )
    out_specs = (P(("dp", "row"), "col"), P("col"), P(None, "row"), P(None, "col"))

    return jax.shard_map(
        per_device, mesh=mesh, in_specs=in_specs, out_specs=out_specs, check_vma=False
    )
```

time: 367 us -> 155 us (0.42)
  waiting for transfers between devices: 217 us -> 64.3 us
  blocking collectives: 87.8 us -> 0 us
  matrix products: 42.5 us -> 2.62 us
  starting transfers between devices: 0.24 us -> 36 us
  Pallas kernels: 0 us -> 29.2 us
  between operations: 14.3 us -> 1.01 us
  other arithmetic: 2.55 us -> 13.1 us
  local copies, waits for them, and re-layouts: 1.64 us -> 7.86 us
    psum x3 -> x0, waiting for transfers between devices: 131 us -> none  [the longest x1 71.9 us: per_device(): lax.psum(row_term + first_group * norm_term, ('dp', 'col'))]
    psum x3 -> x0, blocking collectives: 87.8 us -> none  [the longest x1 69.2 us: per_device(): backward_rows = lax.psum(padded, ('row', 'col')).astype(jnp.bfloat16)]
    all_gather x1 -> x0, waiting for transfers between devices: 85.1 us -> none  [per_device(): portion = lax.all_gather(tokens, 'col', axis=0, tiled=True)]
    ppermute x0 -> x29, waiting for transfers between devices: none -> 64.3 us  [the longest x10 32.7 us: chain_steps(): moved.append(lax.ppermute(piece, 'col', pairs))]
    ppermute x0 -> x29, starting transfers between devices: none -> 36 us  [the longest x19 18.9 us: exchange(): return lax.ppermute(value, axis, pairs)]
    pallas_call x0 -> x6, Pallas kernels: none -> 29.2 us  [the longest x5 24.6 us: block_step(): pl.pallas_call(functools.partial(block_kernel, at, choices, parts, first)...]
    dot_general x4 -> x0, matrix products: 23.1 us -> none  [the longest x1 14.4 us: per_device(): jnp.dot(portion, frozen_weight, preferred_element_type=jnp.float32)]
    dot_general x8 -> x2, matrix products: 19.1 us -> 2.41 us  [contract_product(): lax.dot_general(left, right, (((left_dim,), (right_dim,)), ((), ())), pre...]
  transfers between devices with their start and end apart: 6 -> 29, of which waited for: 4 -> 15; matrix products, arithmetic and copies ran while one was open for 11% -> 11% of each run, Pallas kernels for 0% -> 16%
where the time goes in v1:
time: 155 us; the launch traced here: 154 us
  waiting for transfers between devices  64.3 us (41%)
  starting transfers between devices  36 us (23%)
  Pallas kernels  29.2 us (19%)
  other arithmetic  13.1 us (8%)
  local copies, waits for them, and re-layouts  7.86 us (5%)
  matrix products  2.62 us (2%)
    ppermute x10, waiting for transfers between devices, chain_steps(): moved.append(lax.ppermute(piece, 'col', pairs))  32.7 us
    ppermute x19, waiting for transfers between devices, exchange(): return lax.ppermute(value, axis, pairs)  31.6 us
    pallas_call x5, Pallas kernels, block_step(): pl.pallas_call(functools.partial(block_kernel, at, choices, parts, first)...  24.6 us
    ppermute x19, starting transfers between devices, exchange(): return lax.ppermute(value, axis, pairs)  18.9 us
    ppermute x10, starting transfers between devices, chain_steps(): moved.append(lax.ppermute(piece, 'col', pairs))  17.1 us
    concatenate x4, other arithmetic, per_device(): held = jnp.concatenate([held, exchange(held, 'row', bit)], axis=0)  8.74 us
    pallas_call x1, Pallas kernels, prepare(): pl.pallas_call(prepare_kernel, grid=(columns // tile,), in_specs=[pl.Bloc...  4.62 us
    unnamed x18, local copies, waits for them, and re-layouts  4.46 us
  transfers between devices with their start and end apart: 29, of which 15 were waited for; matrix products, arithmetic and copies ran while one was open for 11% of the time, Pallas kernels for 16%

profile of v1, /device:TPU:0, one launch (start us, length us, event | category | flops | bytes accessed | tf_op | source)
XLA Modules:
  0.0 154.2 jit_solution(12684085565043279009)
XLA Ops:
  0.7 1.4 fusion.9
  2.0 3.1 %collective-permute-start.13 = (bf16[128,2048]{1,0:T(8,128)(2,1)S(1)}, bf16[128,2048]{1,0:T(8,128)(2,1)S(1)}, u32[]{:S(2)}, u32[]{:S(2)}) collective-permute-start(bf16[128,2048]{1,0:T(8,128)(2,1)S(1)} %get-tuple-element.59.refs_3_), channel_id=1, source_target_pairs={{0,1},{1,0},{2,3},{3,2},{4,5},{5,4},{6,7},{7,6},{8,9},{9,8},{10,11... | collective-permute-start | bytes 1572872 | tf_op jit(solution)/shard_map/ppermute | solution.py:260
  5.8 0.9 slice_bitcast_fusion.1
  6.7 1.5 collective-permute-start.11
  8.8 3.4 %copy-done = bf16[2048,2048]{1,0:T(8,128)(2,1)S(1)} copy-done((bf16[2048,2048]{1,0:T(8,128)(2,1)S(1)}, bf16[2048,2048]{1,0:T(8,128)(2,1)}, u32[]{:S(2)}) %copy-start) | copy-done | bytes 8388632
  12.2 4.6 %prepare.1 = (f32[1,2048]{1,0:T(1,128)S(1)}, f32[16,2048]{1,0:T(8,128)S(1)}) custom-call(bf16[2048,2048]{1,0:T(8,128)(2,1)S(1)} %copy-done, bf16[16,2048]{1,0:T(8,128)(2,1)S(1)} %copy-done.3, bf16[16,2048]{1,0:T(8,128)(2,1)S(1)} %copy-done.2), custom_call_target="tpu_custom_call" | custom-call | flops 6000000000 | bytes 8388608 | tf_op jit(solution)/shard_map/prepare/pallas_call | solution.py:89
  16.9 4.7 %collective-permute-done.11 = bf16[1,128,2048]{2,1,0:T(8,128)(2,1)S(1)} collective-permute-done((bf16[1,128,2048]{2,1,0:T(8,128)(2,1)S(1)}, bf16[1,128,2048]{2,1,0:T(8,128)(2,1)S(1)}, u32[]{:S(2)}, u32[]{:S(2)}) %collective-permute-start.11) | collective-permute-done | bytes 524320 | tf_op jit(solution)/shard_map/ppermute | solution.py:25
  21.5 0.8 copy-done.6
  22.4 4.4 %collective-permute-start = (bf16[128,2048]{1,0:T(8,128)(2,1)S(1)}, bf16[128,2048]{1,0:T(8,128)(2,1)S(1)}, u32[]{:S(2)}, u32[]{:S(2)}) collective-permute-start(bf16[128,2048]{1,0:T(8,128)(2,1)S(1)} %get-tuple-element.58.refs_2_), channel_id=1, source_target_pairs={{0,1},{1,0},{2,3},{3,2},{4,5},{5,4},{6,7},{7,6},{8,9},{9,8},{10,11... | collective-permute-start | bytes 1572872 | tf_op jit(solution)/shard_map/ppermute | solution.py:260
  26.7 2.1 %pad_maximum_fusion.3 = bf16[2,128,2048]{2,1,0:T(8,128)(2,1)} fusion(bf16[1,128,2048]{2,1,0:T(8,128)(2,1)} %copy-done.6, bf16[1,128,2048]{2,1,0:T(8,128)(2,1)S(1)} %get-tuple-element.57), kind=kLoop, calls=%fused_computation.6 | loop fusion | flops 524288 | bytes 2097152 | tf_op jit(solution)/shard_map/concatenate | solution.py:304
  29.5 1.9 %collective-permute-done.5 = bf16[1,128,2048]{2,1,0:T(8,128)(2,1)} collective-permute-done((bf16[1,128,2048]{2,1,0:T(8,128)(2,1)}, bf16[1,128,2048]{2,1,0:T(8,128)(2,1)}, u32[]{:S(2)}, u32[]{:S(2)}) %collective-permute-start.5) | collective-permute-done | bytes 524320 | tf_op jit(solution)/shard_map/ppermute | solution.py:25
  31.5 1.5 collective-permute-start.4
  33.0 2.3 %pad_maximum_fusion.2 = bf16[2,128,2048]{2,1,0:T(8,128)(2,1)} fusion(bf16[1,128,2048]{2,1,0:T(8,128)(2,1)} %collective-permute-done.5, bf16[1,128,2048]{2,1,0:T(8,128)(2,1)} %get-tuple-element.56), kind=kLoop, calls=%fused_computation.5 | loop fusion | flops 524288 | bytes 2097152 | tf_op jit(solution)/shard_map/concatenate | solution.py:304
  35.5 1.5 collective-permute-start.7
  37.0 1.5 collective-permute-start.1
  38.5 0.7 collective-permute-start.16
  39.4 1.3 collective-permute-start.10
  40.7 1.3 collective-permute-start.9
  42.0 1.3 collective-permute-start.2
  43.4 1.5 collective-permute-start.17
  44.9 1.9 %pad_maximum_fusion.1.refs_9_.refs_11_.refs_8_ = bf16[4,128,2048]{2,1,0:T(8,128)(2,1)S(1)} fusion(bf16[2,128,2048]{2,1,0:T(8,128)(2,1)} %collective-permute-done.12, bf16[1,128,2048]{2,1,0:T(8,128)(2,1)} %copy-done.6, bf16[1,128,2048]{2,1,0:T(8,128)(2,1)} %copy-done.5), kind=kLoop, calls=%fused_computation.2 | loop fusion | flops 2097152 | bytes 4194304 | tf_op jit(solution)/shard_map/concatenate | solution.py:304
  46.7 2.5 %pad_maximum_fusion.refs_8_.refs_10_ = bf16[4,128,2048]{2,1,0:T(8,128)(2,1)S(1)} fusion(bf16[2,128,2048]{2,1,0:T(8,128)(2,1)} %collective-permute-done.6, bf16[1,128,2048]{2,1,0:T(8,128)(2,1)} %collective-permute-done.5, bf16[1,128,2048]{2,1,0:T(8,128)(2,1)} %get-tuple-element.56), kind=kLoop, calls=%fused_computation.1 | loop fusion | flops 2097152 | bytes 4194304 | tf_op jit(solution)/shard_map/concatenate | solution.py:304
  49.5 5.6 %shard_map.111 = (bf16[4,128,2048]{2,1,0:T(8,128)(2,1)S(1)}, bf16[4,128,2048]{2,1,0:T(8,128)(2,1)S(1)}, f32[1,2048]{1,0:T(1,128)S(1)}, f32[16,2048]{1,0:T(8,128)S(1)}, f32[16,2048]{1,0:T(8,128)S(1)}) custom-call(s32[12]{0:T(128)S(1)} %reshape.20.refs_0_, s32[8]{0:T(128)S(1)} %bitcast.23, bf16[128,2048]{1,0:T(8,128)(2,1)S(1)} %get-tuple-element.58.refs_2_, ...), custom_call_target="tpu_custom_call" | custom-call | flops 2147483648 | bytes 8388608 | tf_op jit(solution)/shard_map/pallas_call | solution.py:211
  55.1 5.7 %shard_map.112 = (bf16[4,128,2048]{2,1,0:T(8,128)(2,1)S(1)}, bf16[4,128,2048]{2,1,0:T(8,128)(2,1)S(1)}, f32[1,2048]{1,0:T(1,128)S(1)}, f32[16,2048]{1,0:T(8,128)S(1)}, f32[16,2048]{1,0:T(8,128)S(1)}) custom-call(s32[12]{0:T(128)S(1)} %reshape.20.refs_0_, ...), custom_call_target="tpu_custom_call", output_to_operand_aliasing={{2}: (10, {}), {3}: (11, {}), {4}: (12, {}), {0}: (13, {}),... | custom-call | flops 2147483648 | bytes 8388608 | tf_op jit(solution)/shard_map/pallas_call | solution.py:211
  60.8 7.9 %collective-permute-done.10.refs_5_ = bf16[128,2048]{1,0:T(8,128)(2,1)S(1)} collective-permute-done((bf16[128,2048]{1,0:T(8,128)(2,1)S(1)}, bf16[128,2048]{1,0:T(8,128)(2,1)S(1)}, u32[]{:S(2)}, u32[]{:S(2)}) %collective-permute-start.10) | collective-permute-done | bytes 524320 | tf_op jit(solution)/shard_map/ppermute | solution.py:260
  68.7 11.5 %collective-permute-done.9.refs_4_ = bf16[128,2048]{1,0:T(8,128)(2,1)S(1)} collective-permute-done((bf16[128,2048]{1,0:T(8,128)(2,1)}, bf16[128,2048]{1,0:T(8,128)(2,1)S(1)}, u32[]{:S(2)}, u32[]{:S(2)}) %collective-permute-start.9) | collective-permute-done | bytes 524320 | tf_op jit(solution)/shard_map/ppermute | solution.py:260
  80.2 5.6 %shard_map.113 = (bf16[4,128,2048]{2,1,0:T(8,128)(2,1)S(1)}, bf16[4,128,2048]{2,1,0:T(8,128)(2,1)S(1)}, f32[1,2048]{1,0:T(1,128)S(1)}, f32[16,2048]{1,0:T(8,128)S(1)}, f32[16,2048]{1,0:T(8,128)S(1)}) custom-call(s32[12]{0:T(128)S(1)} %reshape.20.refs_0_, ...), custom_call_target="tpu_custom_call", output_to_operand_aliasing={{2}: (12, {}), {3}: (13, {}), {4}: (14, {}), {0}: (15, {}),... | custom-call | flops 2147483648 | bytes 8388608 | tf_op jit(solution)/shard_map/pallas_call | solution.py:211
  85.9 6.4 %collective-permute-done.2.refs_3_ = bf16[128,2048]{1,0:T(8,128)(2,1)S(1)} collective-permute-done((bf16[128,2048]{1,0:T(8,128)(2,1)}, bf16[128,2048]{1,0:T(8,128)(2,1)S(1)}, u32[]{:S(2)}, u32[]{:S(2)}) %collective-permute-start.2) | collective-permute-done | bytes 524320 | tf_op jit(solution)/shard_map/ppermute | solution.py:260
  92.3 3.7 %shard_map.114 = (bf16[4,128,2048]{2,1,0:T(8,128)(2,1)S(1)}, f32[1,2048]{1,0:T(1,128)S(1)}, f32[16,2048]{1,0:T(8,128)S(1)}, f32[16,2048]{1,0:T(8,128)S(1)}) custom-call(s32[12]{0:T(128)S(1)} %reshape.20.refs_0_, s32[8]{0:T(128)S(1)} %bitcast.26, ...), custom_call_target="tpu_custom_call", output_to_operand_aliasing={{1}: (9, {}), {2}: (10, {}), {3}: (11, {}), {0}: (12, {})} | custom-call | flops 1073741824 | bytes 8388608 | tf_op jit(solution)/shard_map/pallas_call | solution.py:211
  96.0 6.6 %collective-permute-done.17.refs_3_ = bf16[128,2048]{1,0:T(8,128)(2,1)S(1)} collective-permute-done((bf16[128,2048]{1,0:T(8,128)(2,1)S(1)}, bf16[128,2048]{1,0:T(8,128)(2,1)S(1)}, u32[]{:S(2)}, u32[]{:S(2)}) %collective-permute-start.17) | collective-permute-done | bytes 524320 | tf_op jit(solution)/shard_map/ppermute | solution.py:260
  102.6 3.9 %shard_map.115 = (bf16[4,128,2048]{2,1,0:T(8,128)(2,1)S(1)}, f32[1,2048]{1,0:T(1,128)S(1)}, f32[16,2048]{1,0:T(8,128)S(1)}, f32[16,2048]{1,0:T(8,128)S(1)}) custom-call(s32[12]{0:T(128)S(1)} %reshape.20.refs_0_, s32[8]{0:T(128)S(1)} %bitcast.27, ...), custom_call_target="tpu_custom_call", output_to_operand_aliasing={{1}: (9, {}), {2}: (10, {}), {3}: (11, {}), {0}: (12, {})} | custom-call | flops 1073741824 | bytes 8388608 | tf_op jit(solution)/shard_map/pallas_call | solution.py:211
  106.6 1.2 collective-permute-done.20
  107.8 1.5 collective-permute-start.21
  109.3 2.2 %collective-permute-done.21 = f32[1,2048]{1,0:T(1,128)S(1)} collective-permute-done((f32[1,2048]{1,0:T(1,128)S(1)}, f32[1,2048]{1,0:T(1,128)S(1)}, u32[]{:S(2)}, u32[]{:S(2)}) %collective-permute-start.21) | collective-permute-done | bytes 8224 | tf_op jit(solution)/shard_map/ppermute | solution.py:25
  111.5 1.6 %collective-permute-start.22 = (f32[1,2048]{1,0:T(1,128)S(1)}, f32[1,2048]{1,0:T(1,128)S(1)}, u32[]{:S(2)}, u32[]{:S(2)}) collective-permute-start(f32[1,2048]{1,0:T(1,128)S(1)} %add.81), channel_id=1, source_target_pairs={{0,16},{16,0},{1,17},{17,1},{2,18},{18,2},{3,19},{19,3},{4,20},{20... | collective-permute-start | bytes 24584 | tf_op jit(solution)/shard_map/ppermute | solution.py:25
  114.5 0.9 collective-permute-done.22
  116.1 2.3 %fusion.3 = f32[16,2048]{1,0:T(8,128)S(1)} fusion(bf16[2048,2048]{1,0:T(8,128)(2,1)S(1)} %copy-done.1, bf16[16,2048]{1,0:T(8,128)(2,1)S(1)} %copy-done.2, f32[2048]{0:T(1024)S(1)} %bitcast.30), kind=kOutput, calls=%fused_computation.20 | convolution fusion | flops 134316032 | bytes 8593408 | tf_op jit(solution)/shard_map/dot_general | solution.py:18
  118.8 5.8 %collective-permute-start.24 = (bf16[16,2048]{1,0:T(8,128)(2,1)S(1)}, bf16[16,2048]{1,0:T(8,128)(2,1)S(1)}, u32[]{:S(2)}, u32[]{:S(2)}) collective-permute-start(bf16[16,2048]{1,0:T(8,128)(2,1)S(1)} %add_convert_fusion.3), channel_id=1, source_target_pairs={{0,1},{1,0},{2,3},{3,2},{4,5},{5,4},{6,7},{7,6},{8,9},{9,8},{10,11... | collective-permute-start | bytes 196616 | tf_op jit(solution)/shard_map/ppermute | solution.py:25
  124.5 1.4 collective-permute-start.27
  126.4 0.7 collective-permute-start.19
  127.6 1.4 collective-permute-start.15
  129.1 1.8 %collective-permute-done.27 = f32[16,2048]{1,0:T(8,128)S(1)} collective-permute-done((f32[16,2048]{1,0:T(8,128)S(1)}, f32[16,2048]{1,0:T(8,128)S(1)}, u32[]{:S(2)}, u32[]{:S(2)}) %collective-permute-start.27) | collective-permute-done | bytes 131104 | tf_op jit(solution)/shard_map/ppermute | solution.py:25
  131.0 1.5 collective-permute-start.28
  132.5 2.0 %collective-permute-done.25 = bf16[16,2048]{1,0:T(8,128)(2,1)S(1)} collective-permute-done((bf16[16,2048]{1,0:T(8,128)(2,1)S(1)}, bf16[16,2048]{1,0:T(8,128)(2,1)S(1)}, u32[]{:S(2)}, u32[]{:S(2)}) %collective-permute-start.25) | collective-permute-done | bytes 65568 | tf_op jit(solution)/shard_map/ppermute | solution.py:25
  135.2 0.8 collective-permute-done.28
  136.7 5.5 %collective-permute-done.19 = bf16[1,128,2048]{2,1,0:T(8,128)(2,1)S(1)} collective-permute-done((bf16[1,128,2048]{2,1,0:T(8,128)(2,1)S(1)}, bf16[1,128,2048]{2,1,0:T(8,128)(2,1)S(1)}, u32[]{:S(2)}, u32[]{:S(2)}) %collective-permute-start.19) | collective-permute-done | bytes 524320 | tf_op jit(solution)/shard_map/ppermute | solution.py:25
  142.2 10.5 %collective-permute-done.15 = bf16[1,128,2048]{2,1,0:T(8,128)(2,1)S(1)} collective-permute-done((bf16[1,128,2048]{2,1,0:T(8,128)(2,1)S(1)}, bf16[1,128,2048]{2,1,0:T(8,128)(2,1)S(1)}, u32[]{:S(2)}, u32[]{:S(2)}) %collective-permute-start.15) | collective-permute-done | bytes 524320 | tf_op jit(solution)/shard_map/ppermute | solution.py:25
  153.1 1.1 pad_maximum_fusion.4
  (68 shorter events, 8.1 us)
Async XLA Ops:
  0.6 5.2 %copy-start.7 = (bf16[256,2048]{1,0:T(8,128)(2,1)S(1)}, bf16[256,2048]{1,0:T(8,128)(2,1)}, u32[]{:S(2)}) copy-start(bf16[256,2048]{1,0:T(8,128)(2,1)} %param.13) | copy-start | bytes 3145732
  0.6 8.1 %copy-start.3 = (bf16[16,2048]{1,0:T(8,128)(2,1)S(1)}, bf16[16,2048]{1,0:T(8,128)(2,1)}, u32[]{:S(2)}) copy-start(bf16[16,2048]{1,0:T(8,128)(2,1)} %refs_5_.7) | copy-start | bytes 196612
  0.7 8.1 %copy-start.2 = (bf16[16,2048]{1,0:T(8,128)(2,1)S(1)}, bf16[16,2048]{1,0:T(8,128)(2,1)}, u32[]{:S(2)}) copy-start(bf16[16,2048]{1,0:T(8,128)(2,1)} %refs_6_.9) | copy-start | bytes 196612
  2.0 35.0 %collective-permute-start.13 = (bf16[128,2048]{1,0:T(8,128)(2,1)S(1)}, bf16[128,2048]{1,0:T(8,128)(2,1)S(1)}, u32[]{:S(2)}, u32[]{:S(2)}) collective-permute-start(bf16[128,2048]{1,0:T(8,128)(2,1)S(1)} %get-tuple-element.59.refs_3_), channel_id=1, source_target_pairs={{0,1},{1,0},{2,3},{3,2},{4,5},{5,4},{6,7},{7,6},{8,9},{9,8},{10,11... | collective-permute-start | bytes 1572872 | tf_op jit(solution)/shard_map/ppermute | solution.py:260
  5.1 33.3 %collective-permute-start.8 = (bf16[128,2048]{1,0:T(8,128)(2,1)S(1)}, bf16[128,2048]{1,0:T(8,128)(2,1)S(1)}, u32[]{:S(2)}, u32[]{:S(2)}) collective-permute-start(bf16[128,2048]{1,0:T(8,128)(2,1)S(1)} %get-tuple-element.59.refs_3_), channel_id=1, source_target_pairs={{1,2},{2,1},{5,6},{6,5},{9,10},{10,9},{13,14},{14,13},{17,18},{18,... | collective-permute-start | bytes 1572872 | tf_op jit(solution)/shard_map/ppermute | solution.py:260
  6.7 20.0 %copy-start.5 = (bf16[1,128,2048]{2,1,0:T(8,128)(2,1)}, bf16[1,128,2048]{2,1,0:T(8,128)(2,1)S(1)}, u32[]{:S(2)}) copy-start(bf16[1,128,2048]{2,1,0:T(8,128)(2,1)S(1)} %get-tuple-element.57) | copy-start | bytes 1572868
  6.7 14.8 %collective-permute-start.11 = (bf16[1,128,2048]{2,1,0:T(8,128)(2,1)S(1)}, bf16[1,128,2048]{2,1,0:T(8,128)(2,1)S(1)}, u32[]{:S(2)}, u32[]{:S(2)}) collective-permute-start(bf16[1,128,2048]{2,1,0:T(8,128)(2,1)S(1)} %get-tuple-element.57), channel_id=1, source_target_pairs={{0,8},{4,12},{8,0},{12,4},{1,9},{5,13},{9,1},{13,5},{2,10},{6,14},... | collective-permute-start | bytes 1572872 | tf_op jit(solution)/shard_map/ppermute | solution.py:25
  8.2 23.2 %collective-permute-start.5 = (bf16[1,128,2048]{2,1,0:T(8,128)(2,1)}, bf16[1,128,2048]{2,1,0:T(8,128)(2,1)}, u32[]{:S(2)}, u32[]{:S(2)}) collective-permute-start(bf16[1,128,2048]{2,1,0:T(8,128)(2,1)} %get-tuple-element.56), channel_id=1, source_target_pairs={{0,8},{4,12},{8,0},{12,4},{1,9},{5,13},{9,1},{13,5},{2,10},{6,14},... | collective-permute-start | bytes 1572872 | tf_op jit(solution)/shard_map/ppermute | solution.py:25
  8.8 3.4 %copy-start = (bf16[2048,2048]{1,0:T(8,128)(2,1)S(1)}, bf16[2048,2048]{1,0:T(8,128)(2,1)}, u32[]{:S(2)}) copy-start(bf16[2048,2048]{1,0:T(8,128)(2,1)} %refs_4_.7) | copy-start | bytes 25165828
  16.8 12.0 %collective-permute-start.3 = (f32[1,2048]{1,0:T(1,128)S(1)}, f32[1,2048]{1,0:T(1,128)S(1)}, u32[]{:S(2)}, u32[]{:S(2)}) collective-permute-start(f32[1,2048]{1,0:T(1,128)S(1)} %get-tuple-element.29), channel_id=1, source_target_pairs={{0,4},{4,0},{8,12},{12,8},{1,5},{5,1},{9,13},{13,9},{2,6},{6,2},{1... | collective-permute-start | bytes 24584 | tf_op jit(solution)/shard_map/ppermute | solution.py:25
  21.5 0.8 copy-start.6
  22.4 17.0 %copy-start.8 = (f32[2048]{0:T(1024)S(1)}, f32[2048]{0:T(1024)}, u32[]{:S(2)}) copy-start(f32[2048]{0:T(1024)} %param.12) | copy-start | bytes 24580
  22.4 13.2 %collective-permute-start = (bf16[128,2048]{1,0:T(8,128)(2,1)S(1)}, bf16[128,2048]{1,0:T(8,128)(2,1)S(1)}, u32[]{:S(2)}, u32[]{:S(2)}) collective-permute-start(bf16[128,2048]{1,0:T(8,128)(2,1)S(1)} %get-tuple-element.58.refs_2_), channel_id=1, source_target_pairs={{0,1},{1,0},{2,3},{3,2},{4,5},{5,4},{6,7},{7,6},{8,9},{9,8},{10,11... | collective-permute-start | bytes 1572872 | tf_op jit(solution)/shard_map/ppermute | solution.py:260
  28.8 14.5 %collective-permute-start.12 = (bf16[2,128,2048]{2,1,0:T(8,128)(2,1)}, bf16[2,128,2048]{2,1,0:T(8,128)(2,1)}, u32[]{:S(2)}, u32[]{:S(2)}) collective-permute-start(bf16[2,128,2048]{2,1,0:T(8,128)(2,1)} %pad_maximum_fusion.3), channel_id=1, source_target_pairs={{0,4},{4,0},{8,12},{12,8},{1,5},{5,1},{9,13},{13,9},{2,6},{6,2},{1... | collective-permute-start | bytes 3145736 | tf_op jit(solution)/shard_map/ppermute | solution.py:25
  31.5 3.8 %collective-permute-start.4 = (f32[1,2048]{1,0:T(1,128)S(1)}, f32[1,2048]{1,0:T(1,128)S(1)}, u32[]{:S(2)}, u32[]{:S(2)}) collective-permute-start(f32[1,2048]{1,0:T(1,128)S(1)} %add.72), channel_id=1, source_target_pairs={{0,8},{4,12},{8,0},{12,4},{1,9},{5,13},{9,1},{13,5},{2,10},{6,14},... | collective-permute-start | bytes 24584 | tf_op jit(solution)/shard_map/ppermute | solution.py:25
  35.2 11.5 %collective-permute-start.6 = (bf16[2,128,2048]{2,1,0:T(8,128)(2,1)}, bf16[2,128,2048]{2,1,0:T(8,128)(2,1)}, u32[]{:S(2)}, u32[]{:S(2)}) collective-permute-start(bf16[2,128,2048]{2,1,0:T(8,128)(2,1)} %pad_maximum_fusion.2), channel_id=1, source_target_pairs={{0,4},{4,0},{8,12},{12,8},{1,5},{5,1},{9,13},{13,9},{2,6},{6,2},{1... | collective-permute-start | bytes 3145736 | tf_op jit(solution)/shard_map/ppermute | solution.py:25
  35.5 3.9 %collective-permute-start.7 = (bf16[128,2048]{1,0:T(8,128)(2,1)S(1)}, bf16[128,2048]{1,0:T(8,128)(2,1)}, u32[]{:S(2)}, u32[]{:S(2)}) collective-permute-start(bf16[128,2048]{1,0:T(8,128)(2,1)S(1)} %get-tuple-element.58.refs_2_), channel_id=1, source_target_pairs={{1,2},{2,1},{5,6},{6,5},{9,10},{10,9},{13,14},{14,13},{17,18},{18,... | collective-permute-start | bytes 1572872 | tf_op jit(solution)/shard_map/ppermute | solution.py:260
  37.0 3.7 %collective-permute-start.1 = (bf16[128,2048]{1,0:T(8,128)(2,1)S(1)}, bf16[128,2048]{1,0:T(8,128)(2,1)}, u32[]{:S(2)}, u32[]{:S(2)}) collective-permute-start(bf16[128,2048]{1,0:T(8,128)(2,1)S(1)} %collective-permute-done.refs_2_), channel_id=1, source_target_pairs={{1,2},{2,1},{5,6},{6,5},{9,10},{10,9},{13,14},{14,13},{17,18},{18,... | collective-permute-start | bytes 1572872 | tf_op jit(solution)/shard_map/ppermute | solution.py:260
  38.5 3.6 %collective-permute-start.16 = (bf16[128,2048]{1,0:T(8,128)(2,1)S(1)}, bf16[128,2048]{1,0:T(8,128)(2,1)S(1)}, u32[]{:S(2)}, u32[]{:S(2)}) collective-permute-start(bf16[128,2048]{1,0:T(8,128)(2,1)S(1)} %collective-permute-done.13.refs_3_), channel_id=1, source_target_pairs={{1,2},{2,1},{5,6},{6,5},{9,10},{10,9},{13,14},{14,13},{17,18},{18,... | collective-permute-start | bytes 1572872 | tf_op jit(solution)/shard_map/ppermute | solution.py:260
  39.4 29.2 %collective-permute-start.10 = (bf16[128,2048]{1,0:T(8,128)(2,1)S(1)}, bf16[128,2048]{1,0:T(8,128)(2,1)S(1)}, u32[]{:S(2)}, u32[]{:S(2)}) collective-permute-start(bf16[128,2048]{1,0:T(8,128)(2,1)S(1)} %collective-permute-done.8.refs_3_), channel_id=1, source_target_pairs={{1,0},{2,3},{5,4},{6,7},{9,8},{10,11},{13,12},{14,15},{17,16},{18,... | collective-permute-start | bytes 1572872 | tf_op jit(solution)/shard_map/ppermute | solution.py:260
  40.7 39.5 %collective-permute-start.9 = (bf16[128,2048]{1,0:T(8,128)(2,1)}, bf16[128,2048]{1,0:T(8,128)(2,1)S(1)}, u32[]{:S(2)}, u32[]{:S(2)}) collective-permute-start(bf16[128,2048]{1,0:T(8,128)(2,1)} %collective-permute-done.7.refs_2_), channel_id=1, source_target_pairs={{1,0},{2,3},{5,4},{6,7},{9,8},{10,11},{13,12},{14,15},{17,16},{18,... | collective-permute-start | bytes 1572872 | tf_op jit(solution)/shard_map/ppermute | solution.py:260
  42.0 50.2 %collective-permute-start.2 = (bf16[128,2048]{1,0:T(8,128)(2,1)}, bf16[128,2048]{1,0:T(8,128)(2,1)S(1)}, u32[]{:S(2)}, u32[]{:S(2)}) collective-permute-start(bf16[128,2048]{1,0:T(8,128)(2,1)} %collective-permute-done.1.refs_2_), channel_id=1, source_target_pairs={{1,0},{2,3},{5,4},{6,7},{9,8},{10,11},{13,12},{14,15},{17,16},{18,... | collective-permute-start | bytes 1572872 | tf_op jit(solution)/shard_map/ppermute | solution.py:260
  43.4 59.2 %collective-permute-start.17 = (bf16[128,2048]{1,0:T(8,128)(2,1)S(1)}, bf16[128,2048]{1,0:T(8,128)(2,1)S(1)}, u32[]{:S(2)}, u32[]{:S(2)}) collective-permute-start(bf16[128,2048]{1,0:T(8,128)(2,1)S(1)} %collective-permute-done.16.refs_2_), channel_id=1, source_target_pairs={{1,0},{2,3},{5,4},{6,7},{9,8},{10,11},{13,12},{14,15},{17,16},{18,... | collective-permute-start | bytes 1572872 | tf_op jit(solution)/shard_map/ppermute | solution.py:260
  44.8 4.6 %copy-start.1 = (bf16[2048,2048]{1,0:T(8,128)(2,1)S(1)}, bf16[2048,2048]{1,0:T(8,128)(2,1)}, u32[]{:S(2)}) copy-start(bf16[2048,2048]{1,0:T(8,128)(2,1)} %refs_4_.7) | copy-start | bytes 25165828
  46.7 2.8 %copy-start.4 = (s32[1,8]{1,0:T(1,128)S(1)}, s32[1,8]{1,0:T(1,128)}, u32[]{:S(2)}) copy-start(s32[1,8]{1,0:T(1,128)} %param.14) | copy-start | bytes 100
  106.5 1.2 collective-permute-start.20
  107.8 3.7 %collective-permute-start.21 = (f32[1,2048]{1,0:T(1,128)S(1)}, f32[1,2048]{1,0:T(1,128)S(1)}, u32[]{:S(2)}, u32[]{:S(2)}) collective-permute-start(f32[1,2048]{1,0:T(1,128)S(1)} %add.80), channel_id=1, source_target_pairs={{0,8},{4,12},{8,0},{12,4},{1,9},{5,13},{9,1},{13,5},{2,10},{6,14},... | collective-permute-start | bytes 24584 | tf_op jit(solution)/shard_map/ppermute | solution.py:25
  111.5 3.8 %collective-permute-start.22 = (f32[1,2048]{1,0:T(1,128)S(1)}, f32[1,2048]{1,0:T(1,128)S(1)}, u32[]{:S(2)}, u32[]{:S(2)}) collective-permute-start(f32[1,2048]{1,0:T(1,128)S(1)} %add.81), channel_id=1, source_target_pairs={{0,16},{16,0},{1,17},{17,1},{2,18},{18,2},{3,19},{19,3},{4,20},{20... | collective-permute-start | bytes 24584 | tf_op jit(solution)/shard_map/ppermute | solution.py:25
  113.1 5.6 %collective-permute-start.23 = (f32[16,2048]{1,0:T(8,128)S(1)}, f32[16,2048]{1,0:T(8,128)S(1)}, u32[]{:S(2)}, u32[]{:S(2)}) collective-permute-start(f32[16,2048]{1,0:T(8,128)S(1)} %get-tuple-element.51), channel_id=1, source_target_pairs={{0,16},{16,0},{1,17},{17,1},{2,18},{18,2},{3,19},{19,3},{4,20},{20... | collective-permute-start | bytes 393224 | tf_op jit(solution)/shard_map/ppermute | solution.py:25
  113.7 12.3 %collective-permute-start.18 = (bf16[2,128,2048]{2,1,0:T(8,128)(2,1)S(1)}, bf16[2,128,2048]{2,1,0:T(8,128)(2,1)S(1)}, u32[]{:S(2)}, u32[]{:S(2)}) collective-permute-start(bf16[2,128,2048]{2,1,0:T(8,128)(2,1)S(1)} %slice.53), channel_id=1, source_target_pairs={{0,4},{4,0},{8,12},{12,8},{1,5},{5,1},{9,13},{13,9},{2,6},{6,2},{1... | collective-permute-start | bytes 3145736 | tf_op jit(solution)/shard_map/ppermute | solution.py:25
  113.9 13.2 %collective-permute-start.14 = (bf16[2,128,2048]{2,1,0:T(8,128)(2,1)S(1)}, bf16[2,128,2048]{2,1,0:T(8,128)(2,1)S(1)}, u32[]{:S(2)}, u32[]{:S(2)}) collective-permute-start(bf16[2,128,2048]{2,1,0:T(8,128)(2,1)S(1)} %slice.49), channel_id=1, source_target_pairs={{0,4},{4,0},{8,12},{12,8},{1,5},{5,1},{9,13},{13,9},{2,6},{6,2},{1... | collective-permute-start | bytes 3145736 | tf_op jit(solution)/shard_map/ppermute | solution.py:25
  116.0 8.5 %collective-permute-start.26 = (f32[16,2048]{1,0:T(8,128)S(1)}, f32[16,2048]{1,0:T(8,128)S(1)}, u32[]{:S(2)}, u32[]{:S(2)}) collective-permute-start(f32[16,2048]{1,0:T(8,128)S(1)} %multiply_add_fusion), channel_id=1, source_target_pairs={{0,4},{4,0},{8,12},{12,8},{1,5},{5,1},{9,13},{13,9},{2,6},{6,2},{1... | collective-permute-start | bytes 393224 | tf_op jit(solution)/shard_map/ppermute | solution.py:25
  118.8 10.3 %collective-permute-start.24 = (bf16[16,2048]{1,0:T(8,128)(2,1)S(1)}, bf16[16,2048]{1,0:T(8,128)(2,1)S(1)}, u32[]{:S(2)}, u32[]{:S(2)}) collective-permute-start(bf16[16,2048]{1,0:T(8,128)(2,1)S(1)} %add_convert_fusion.3), channel_id=1, source_target_pairs={{0,1},{1,0},{2,3},{3,2},{4,5},{5,4},{6,7},{7,6},{8,9},{9,8},{10,11... | collective-permute-start | bytes 196616 | tf_op jit(solution)/shard_map/ppermute | solution.py:25
  124.5 6.4 %collective-permute-start.27 = (f32[16,2048]{1,0:T(8,128)S(1)}, f32[16,2048]{1,0:T(8,128)S(1)}, u32[]{:S(2)}, u32[]{:S(2)}) collective-permute-start(f32[16,2048]{1,0:T(8,128)S(1)} %add.89), channel_id=1, source_target_pairs={{0,8},{4,12},{8,0},{12,4},{1,9},{5,13},{9,1},{13,5},{2,10},{6,14},... | collective-permute-start | bytes 393224 | tf_op jit(solution)/shard_map/ppermute | solution.py:25
  126.4 15.8 %collective-permute-start.19 = (bf16[1,128,2048]{2,1,0:T(8,128)(2,1)S(1)}, bf16[1,128,2048]{2,1,0:T(8,128)(2,1)S(1)}, u32[]{:S(2)}, u32[]{:S(2)}) collective-permute-start(bf16[1,128,2048]{2,1,0:T(8,128)(2,1)S(1)} %slice.61), channel_id=1, source_target_pairs={{0,8},{4,12},{8,0},{12,4},{1,9},{5,13},{9,1},{13,5},{2,10},{6,14},... | collective-permute-start | bytes 1572872 | tf_op jit(solution)/shard_map/ppermute | solution.py:25
  127.6 25.1 %collective-permute-start.15 = (bf16[1,128,2048]{2,1,0:T(8,128)(2,1)S(1)}, bf16[1,128,2048]{2,1,0:T(8,128)(2,1)S(1)}, u32[]{:S(2)}, u32[]{:S(2)}) collective-permute-start(bf16[1,128,2048]{2,1,0:T(8,128)(2,1)S(1)} %slice.59), channel_id=1, source_target_pairs={{0,8},{4,12},{8,0},{12,4},{1,9},{5,13},{9,1},{13,5},{2,10},{6,14},... | collective-permute-start | bytes 1572872 | tf_op jit(solution)/shard_map/ppermute | solution.py:25
  129.1 5.5 %collective-permute-start.25 = (bf16[16,2048]{1,0:T(8,128)(2,1)S(1)}, bf16[16,2048]{1,0:T(8,128)(2,1)S(1)}, u32[]{:S(2)}, u32[]{:S(2)}) collective-permute-start(bf16[16,2048]{1,0:T(8,128)(2,1)S(1)} %add_convert_fusion.2), channel_id=1, source_target_pairs={{0,2},{1,3},{2,0},{3,1},{4,6},{5,7},{6,4},{7,5},{8,10},{9,11},{10,... | collective-permute-start | bytes 196616 | tf_op jit(solution)/shard_map/ppermute | solution.py:25
  131.0 5.0 %collective-permute-start.28 = (f32[16,2048]{1,0:T(8,128)S(1)}, f32[16,2048]{1,0:T(8,128)S(1)}, u32[]{:S(2)}, u32[]{:S(2)}) collective-permute-start(f32[16,2048]{1,0:T(8,128)S(1)} %add.90), channel_id=1, source_target_pairs={{0,16},{16,0},{1,17},{17,1},{2,18},{18,2},{3,19},{19,3},{4,20},{20... | collective-permute-start | bytes 393224 | tf_op jit(solution)/shard_map/ppermute | solution.py:25
